TPU v7x, 32 devices: a whole 2x2x4 slice. The times are simulated.
32 devices in a mesh: row: 8 (over z, core), col: 4 (over y, x).
Axes of the slice: x: 2, y: 2, z: 4, core: 2. Of those that a mesh axis runs over, the one named last changes fastest.
Arguments:
- basis: float32 [8192, 1024], P('row', 'col'), may hold values from -6 to 6
- merge_coef: float32 [1024, 4096], P('row', 'col'), may hold values from -0.1875 to 0.1875
- panels: float32 [2, 8192, 256], P(None, ('row', 'col')), may hold values from -0.0625 to 0.0625
- factors: float32 [2, 256, 256], replicated, may hold values from -1 to 1
Outputs:
- vectors: float32 [8192, 4096], P(('row', 'col'))
- wsum: float32 [2, 256], replicated
All inputs are finite; a program needn't handle non-finite values.
Results may differ from a plain program's by a relative error of at most 0.0001.
Values sent between devices are 32-bit elements; how exact they have to be, the bound alone decides.
No kernel may reach another device: no remote copies, remote signals or barrier semaphores. Data moves between devices by JAX's collectives and lax.ppermute only.
A program may use at most 128 MiB of HBM per device.

v0:
```python
import jax
import jax.numpy as jnp
from jax import lax
from jax.sharding import PartitionSpec as P

HI = lax.Precision.HIGHEST


def matmul(left, right):
    return jnp.dot(left, right, precision=HI, preferred_element_type=jnp.float32)


def to_tall(block):
    return lax.all_to_all(block, "col", split_axis=0, concat_axis=1, tiled=True)


def per_device(basis, merge_coef, panels, factors):
    coef = lax.all_gather(merge_coef, "row", axis=0, tiled=True)
    block = matmul(lax.all_gather(basis, "col", axis=1, tiled=True), coef)
    upper = jnp.triu(factors)
    local_v = lax.all_gather(panels, "col", axis=1, tiled=True)

    def reduce_terms(terms):
        return lax.psum(terms, "row")

    field = block
    first = local_v[0]
    second = local_v[1]
    proj_one = reduce_terms(matmul(first.T, field))
    field = field - matmul(first, matmul(upper[0], proj_one))
    proj_two = reduce_terms(matmul(second.T, field))
    field = field - matmul(second, matmul(upper[1], proj_two))
    row_one = jnp.sum(proj_one, axis=1)
    row_two = jnp.sum(proj_two, axis=1)
    row_one, row_two = lax.psum((row_one, row_two), "col")
    field = to_tall(field)
    scale = jnp.sqrt(jnp.float32(field.shape[1]))
    return (field, jnp.stack([row_one, row_two]) / scale)


def solution(mesh):
    placed = (P("row", "col"), P("row", "col"), P(None, ("row", "col"), None), P())
    return jax.shard_map(
        per_device,
        mesh=mesh,
        in_specs=placed,
        out_specs=(P(("row", "col"), None), P()),
        check_vma=False,
    )
```

profile of v0, /device:TPU:0, one launch (start us, length us, event | category | flops | bytes accessed | tf_op | source)
XLA Modules:
  0.0 370.3 jit_solution(15266776425502628769)
XLA Ops:
  7.2 0.0 all-gather.4.cloned.1.call-start
  7.2 0.7 all-gather.4.cloned.1.call-update
  7.9 0.0 all-gather.6.cloned.1.call-start
  7.9 0.7 all-gather.6.cloned.1.call-update
  8.6 0.0 all-gather.8.cloned.1.call-start
  8.7 0.7 all-gather.8.cloned.1.call-update
  9.4 0.0 all-reduce.4.cloned.1.call-start
  9.4 55.6 %all-gather.4.cloned.1.call-done = f32[1024,1024]{1,0:T(8,128)} async-done(((f32[1024,256]{1,0:T(8,128)}), f32[1024,1024]{1,0:T(8,128)}) %all-gather.4.cloned.1.call-update) | async-done | bytes 4194320 | tf_op jit(solution)/shard_map/all_gather | solution.py:19
  65.0 48.5 %all-gather.6.cloned.1.call-done = f32[1024,1024]{1,0:T(8,128)} async-done(((f32[128,1024]{1,0:T(8,128)}), f32[1024,1024]{1,0:T(8,128)}) %all-gather.6.cloned.1.call-update) | async-done | bytes 4194320 | tf_op jit(solution)/shard_map/all_gather | solution.py:18
  113.5 17.5 %fusion.2 = f32[1024,1024]{1,0:T(8,128)} fusion(f32[1024,1024]{1,0:T(8,128)} %all-gather.4.cloned.1.call-done, f32[1024,1024]{1,0:T(8,128)} %all-gather.6.cloned.1.call-done), kind=kOutput, calls=%fused_computation.14 | convolution fusion | flops 12884901888 | bytes 12582912 | tf_op jit(solution)/shard_map/dot_general | solution.py:10
  131.0 0.0 copy-start.4
  131.0 18.4 %all-gather.8.cloned.1.call-done = f32[2,1024,256]{2,1,0:T(8,128)} async-done(((f32[2,256,256]{2,1,0:T(8,128)}), f32[2,1024,256]{2,1,0:T(8,128)}) %all-gather.8.cloned.1.call-update) | async-done | bytes 2097168 | tf_op jit(solution)/shard_map/all_gather | solution.py:21
  149.4 0.0 copy-start.1
  149.4 10.3 %convolution_bitcast_fusion.1 = f32[256,1024]{0,1:T(8,128)} fusion(f32[1024,1024]{1,0:T(8,128)} %fusion.2, f32[2,1024,256]{2,1,0:T(8,128)} %all-gather.8.cloned.1.call-done), kind=kOutput, calls=%fused_computation.3 | convolution fusion | flops 3221225472 | bytes 6291456 | tf_op jit(solution)/shard_map/dot_general | solution.py:10
  159.7 0.0 all-reduce.4.cloned.1.call-update
  159.7 0.0 all-reduce.6.cloned.1.call-start
  159.8 0.1 iota_compare_fusion
  159.9 0.0 copy-done.4
  159.9 0.1 broadcast_select_fusion
  159.9 59.2 %all-reduce.4.cloned.1.call-done = f32[256,1024]{0,1:T(8,128)} async-done(((f32[256,1024]{0,1:T(8,128)}), f32[256,1024]{0,1:T(8,128)}) %all-reduce.4.cloned.1.call-update) | async-done | bytes 1048592 | tf_op jit(solution)/shard_map/psum | solution.py:24
  219.2 2.3 fusion.1
  221.4 0.0 copy-done.1
  221.4 5.7 %bitcast_subtract_fusion.1 = f32[1024,1024]{1,0:T(8,128)S(1)} fusion(f32[1024,1024]{1,0:T(8,128)} %fusion.2, f32[256,1024]{1,0:T(8,128)S(1)} %fusion.1, f32[2,1024,256]{2,1,0:T(8,128)S(1)} %copy-done.1), kind=kOutput, calls=%fused_computation.1 | convolution fusion | flops 3222274048 | bytes 10485760 | tf_op jit(solution)/shard_map/dot_general | solution.py:10
  227.1 0.0 copy-start
  227.1 2.0 copy-done
  229.1 7.8 %convolution_bitcast_fusion = f32[256,1024]{0,1:T(8,128)} fusion(f32[1024,1024]{1,0:T(8,128)S(1)} %bitcast_subtract_fusion.1, f32[2,1024,256]{2,1,0:T(8,128)S(1)} %copy-done.1), kind=kOutput, calls=%fused_computation.2 | convolution fusion | flops 3221225472 | bytes 6291456 | tf_op jit(solution)/shard_map/dot_general | solution.py:10
  237.0 0.0 all-reduce.6.cloned.1.call-update
  237.0 58.5 %all-reduce.6.cloned.1.call-done = f32[256,1024]{0,1:T(8,128)} async-done(((f32[256,1024]{0,1:T(8,128)}), f32[256,1024]{0,1:T(8,128)}) %all-reduce.6.cloned.1.call-update) | async-done | bytes 1048592 | tf_op jit(solution)/shard_map/psum | solution.py:24
  295.5 2.3 fusion
  297.7 6.7 %bitcast_subtract_fusion = f32[1024,1024]{1,0:T(8,128)} fusion(f32[1024,1024]{1,0:T(8,128)} %copy-done, f32[256,1024]{1,0:T(8,128)S(1)} %fusion, f32[2,1024,256]{2,1,0:T(8,128)S(1)} %copy-done.1), kind=kOutput, calls=%fused_computation | convolution fusion | flops 3222274048 | bytes 10485760 | tf_op jit(solution)/shard_map/dot_general | solution.py:10
  304.4 0.0 copy-start.2
  304.4 0.0 copy-start.3
  304.4 5.0 %all-to-all-start = ((f32[4,256,1024]{2,1,0:T(8,128)}), f32[4,256,1024]{2,1,0:T(8,128)}, u32[]{:S(2)}, u32[]{:S(2)}) async-start(f32[4,256,1024]{2,1,0:T(8,128)} %bitcast.36), calls=%async_computation | async-start | bytes 8388608 | tf_op jit(solution)/shard_map/all_to_all | solution.py:14
  309.4 0.0 copy-done.2
  309.4 0.2 reduce_sum.18
  309.6 0.0 copy-done.3
  309.6 0.2 reduce_sum.19
  309.7 48.7 %all-reduce = (f32[1,256]{1,0:T(1,128)S(1)}, f32[1,256]{1,0:T(1,128)S(1)}) all-reduce(f32[1,256]{1,0:T(1,128)S(1)} %bitcast.39, f32[1,256]{1,0:T(1,128)S(1)} %bitcast.38), channel_id=1, replica_groups=mesh['row'=8,'col'=4] {'col'}, use_global_device_ids=true, to_apply=%region_5.6 | all-reduce | flops 512 | bytes 4096 | tf_op jit(solution)/shard_map/psum | solution.py:35
  358.4 0.6 maximum_multiply_fusion
  359.0 0.0 all-to-all-done
  359.0 4.8 %copy.7 = f32[4,32,8,1024]{3,2,0,1:T(8,128)} copy(f32[4,32,8,1024]{3,2,1,0:T(8,128)} %bitcast.12) | data formatting | bytes 8388608 | tf_op jit(solution)/shard_map/all_to_all | solution.py:14
  (1 shorter events, 0.0 us)
Async XLA Ops:
  7.2 57.8 %all-gather.4.cloned.1.call-start = ((), (), s32[]{:S(2)}) async-start(), calls=%async_computation.1 | async-start | bytes 5242880 | tf_op jit(solution)/shard_map/all_gather | solution.py:19
  7.9 105.6 %all-gather.6.cloned.1.call-start = ((), (), s32[]{:S(2)}) async-start(), calls=%async_computation.2 | async-start | bytes 4718592 | tf_op jit(solution)/shard_map/all_gather | solution.py:18
  8.6 140.7 %all-gather.8.cloned.1.call-start = ((), (), s32[]{:S(2)}) async-start(), calls=%async_computation.3 | async-start | bytes 2621440 | tf_op jit(solution)/shard_map/all_gather | solution.py:21
  9.4 209.8 %all-reduce.4.cloned.1.call-start = ((), (), s32[]{:S(2)}) async-start(), calls=%async_computation.4 | async-start | bytes 2097152 | tf_op jit(solution)/shard_map/psum | solution.py:24
  131.0 28.9 %copy-start.4 = (f32[2,256,256]{2,1,0:T(8,128)S(1)}, f32[2,256,256]{2,1,0:T(8,128)}, u32[]{:S(2)}) copy-start(f32[2,256,256]{2,1,0:T(8,128)} %param.7) | copy-start | bytes 1572868
  149.4 72.1 %copy-start.1 = (f32[2,1024,256]{2,1,0:T(8,128)S(1)}, f32[2,1024,256]{2,1,0:T(8,128)}, u32[]{:S(2)}) copy-start(f32[2,1024,256]{2,1,0:T(8,128)} %all-gather.8.cloned.1.call-done) | copy-start | bytes 6291460
  159.7 135.8 %all-reduce.6.cloned.1.call-start = ((), (), s32[]{:S(2)}) async-start(), calls=%async_computation.5 | async-start | bytes 2097152 | tf_op jit(solution)/shard_map/psum | solution.py:24
  227.1 2.0 copy-start
  304.4 5.0 %copy-start.2 = (f32[256,1024]{0,1:T(8,128)S(1)}, f32[256,1024]{0,1:T(8,128)}, u32[]{:S(2)}) copy-start(f32[256,1024]{0,1:T(8,128)} %all-reduce.4.cloned.1.call-done) | copy-start | bytes 3145732
  304.4 5.1 %copy-start.3 = (f32[256,1024]{0,1:T(8,128)S(1)}, f32[256,1024]{0,1:T(8,128)}, u32[]{:S(2)}) copy-start(f32[256,1024]{0,1:T(8,128)} %all-reduce.6.cloned.1.call-done) | copy-start | bytes 3145732
  304.4 54.5 %all-to-all-start = ((f32[4,256,1024]{2,1,0:T(8,128)}), f32[4,256,1024]{2,1,0:T(8,128)}, u32[]{:S(2)}, u32[]{:S(2)}) async-start(f32[4,256,1024]{2,1,0:T(8,128)} %bitcast.36), calls=%async_computation | async-start | bytes 8388608 | tf_op jit(solution)/shard_map/all_to_all | solution.py:14
Sparse Core Ops, SparseCore 0:
  9.8 55.1 all-gather.3
  66.6 46.8 all-gather.5
  115.3 33.9 all-gather.7
  159.8 59.2 all-reduce.3
  237.1 58.2 all-reduce.5
where the time goes:
time: 371 us; the launch traced here: 370 us
  waiting for transfers between devices  242 us (65%)
  matrix products  52.5 us (14%)
  blocking collectives  48.7 us (13%)
  between operations  13.9 us (4%)
  local copies, waits for them, and re-layouts  6.81 us (2%)
  starting transfers between devices  5.16 us (1%)
    psum x2, waiting for transfers between devices, reduce_terms(): return lax.psum(terms, 'row')  118 us
    all_gather x1, waiting for transfers between devices, per_device(): block = matmul(lax.all_gather(basis, 'col', axis=1, tiled=True), coef)  55.6 us
    dot_general x7, matrix products, matmul(): jnp.dot(left, right, precision=HI, preferred_element_type=jnp.float32)  52.5 us
    psum x1, blocking collectives, per_device(): row_one, row_two = lax.psum((row_one, row_two), 'col')  48.7 us
    all_gather x1, waiting for transfers between devices, per_device(): coef = lax.all_gather(merge_coef, 'row', axis=0, tiled=True)  48.5 us
    all_gather x1, waiting for transfers between devices, per_device(): local_v = lax.all_gather(panels, 'col', axis=1, tiled=True)  18.4 us
  transfers between devices with their start and end apart: 6, of which 5 were waited for; matrix products, arithmetic and copies ran while one was open for 5% of the time, Pallas kernels for 0%

commit v1 on v0

--- a/solution.py
+++ b/solution.py
@@ -16,7 +16,7 @@
 
 def per_device(basis, merge_coef, panels, factors):
     coef = lax.all_gather(merge_coef, "row", axis=0, tiled=True)
-    block = matmul(lax.all_gather(basis, "col", axis=1, tiled=True), coef)
+    block = matmul(jnp.concatenate(lax.all_gather(basis, "col"), axis=1), coef)
     upper = jnp.triu(factors)
     local_v = lax.all_gather(panels, "col", axis=1, tiled=True)
 

time: 371 us -> 371 us (level)
  local copies, waits for them, and re-layouts: 6.81 us -> 12.2 us
  waiting for transfers between devices: 242 us -> 237 us
    reshape x0 -> x1, local copies, waits for them, and re-layouts: none -> 5.34 us  [per_device(): block = matmul(jnp.concatenate(lax.all_gather(basis, 'col'), axis=1), coef)]
    all_gather x1, waiting for transfers between devices: 48.5 us -> 43.2 us  [per_device(): coef = lax.all_gather(merge_coef, 'row', axis=0, tiled=True)]
  transfers between devices with their start and end apart: 6 -> 6, of which waited for: 5 -> 5; matrix products, arithmetic and copies ran while one was open for 5% -> 6% of each run, Pallas kernels for 0% -> 0%
where the time goes in v1:
time: 371 us; the launch traced here: 370 us
  waiting for transfers between devices  237 us (64%)
  matrix products  52.6 us (14%)
  blocking collectives  48.7 us (13%)
  between operations  13.9 us (4%)
  local copies, waits for them, and re-layouts  12.2 us (3%)
  starting transfers between devices  5.16 us (1%)
    psum x2, waiting for transfers between devices, reduce_terms(): return lax.psum(terms, 'row')  118 us
    all_gather x1, waiting for transfers between devices, per_device(): block = matmul(jnp.concatenate(lax.all_gather(basis, 'col'), axis=1), coef)  55.7 us
    dot_general x7, matrix products, matmul(): jnp.dot(left, right, precision=HI, preferred_element_type=jnp.float32)  52.6 us
    psum x1, blocking collectives, per_device(): row_one, row_two = lax.psum((row_one, row_two), 'col')  48.7 us
    all_gather x1, waiting for transfers between devices, per_device(): coef = lax.all_gather(merge_coef, 'row', axis=0, tiled=True)  43.2 us
    all_gather x1, waiting for transfers between devices, per_device(): local_v = lax.all_gather(panels, 'col', axis=1, tiled=True)  18.3 us
  transfers between devices with their start and end apart: 6, of which 5 were waited for; matrix products, arithmetic and copies ran while one was open for 6% of the time, Pallas kernels for 0%

profile of v1, /device:TPU:0, one launch (start us, length us, event | category | flops | bytes accessed | tf_op | source)
XLA Modules:
  0.0 370.4 jit_solution(13304061839575053754)
XLA Ops:
  7.2 0.0 all-gather.9.cloned.1.call-start
  7.2 0.7 all-gather.9.cloned.1.call-update
  7.9 0.0 all-gather.5.cloned.1.call-start
  7.9 0.7 all-gather.5.cloned.1.call-update
  8.6 0.0 all-gather.7.cloned.1.call-start
  8.7 0.7 all-gather.7.cloned.1.call-update
  9.4 0.0 all-reduce.4.cloned.1.call-start
  9.4 55.7 %all-gather.9.cloned.1.call-done = f32[4096,256]{1,0:T(8,128)} async-done(((f32[1024,256]{1,0:T(8,128)}), f32[4096,256]{1,0:T(8,128)}) %all-gather.9.cloned.1.call-update) | async-done | bytes 4194320 | tf_op jit(solution)/shard_map/all_gather | solution.py:19
  65.1 5.3 %copy.8 = f32[1024,4,256]{0,2,1:T(8,128)} copy(f32[1024,4,256]{2,0,1:T(8,128)} %bitcast.41) | data formatting | bytes 8388608 | tf_op jit(solution)/shard_map/reshape | solution.py:19
  70.5 43.2 %all-gather.5.cloned.1.call-done = f32[1024,1024]{1,0:T(8,128)} async-done(((f32[128,1024]{1,0:T(8,128)}), f32[1024,1024]{1,0:T(8,128)}) %all-gather.5.cloned.1.call-update) | async-done | bytes 4194320 | tf_op jit(solution)/shard_map/all_gather | solution.py:18
  113.6 17.6 %fusion.2 = f32[1024,1024]{1,0:T(8,128)} fusion(f32[1024,1024]{0,1:T(8,128)} %bitcast.43, f32[1024,1024]{1,0:T(8,128)} %all-gather.5.cloned.1.call-done), kind=kOutput, calls=%fused_computation.14 | convolution fusion | flops 12884901888 | bytes 12582912 | tf_op jit(solution)/shard_map/dot_general | solution.py:10
  131.2 0.0 copy-start.4
  131.2 18.3 %all-gather.7.cloned.1.call-done = f32[2,1024,256]{2,1,0:T(8,128)} async-done(((f32[2,256,256]{2,1,0:T(8,128)}), f32[2,1024,256]{2,1,0:T(8,128)}) %all-gather.7.cloned.1.call-update) | async-done | bytes 2097168 | tf_op jit(solution)/shard_map/all_gather | solution.py:21
  149.5 0.0 copy-start.1
  149.5 10.3 %convolution_bitcast_fusion.1 = f32[256,1024]{0,1:T(8,128)} fusion(f32[1024,1024]{1,0:T(8,128)} %fusion.2, f32[2,1024,256]{2,1,0:T(8,128)} %all-gather.7.cloned.1.call-done), kind=kOutput, calls=%fused_computation.3 | convolution fusion | flops 3221225472 | bytes 6291456 | tf_op jit(solution)/shard_map/dot_general | solution.py:10
  159.8 0.0 all-reduce.4.cloned.1.call-update
  159.8 0.0 all-reduce.6.cloned.1.call-start
  159.9 0.1 iota_compare_fusion
  160.0 0.0 copy-done.4
  160.0 0.1 broadcast_select_fusion
  160.1 59.2 %all-reduce.4.cloned.1.call-done = f32[256,1024]{0,1:T(8,128)} async-done(((f32[256,1024]{0,1:T(8,128)}), f32[256,1024]{0,1:T(8,128)}) %all-reduce.4.cloned.1.call-update) | async-done | bytes 1048592 | tf_op jit(solution)/shard_map/psum | solution.py:24
  219.3 2.3 fusion.1
  221.5 0.0 copy-done.1
  221.6 5.7 %bitcast_subtract_fusion.1 = f32[1024,1024]{1,0:T(8,128)S(1)} fusion(f32[1024,1024]{1,0:T(8,128)} %fusion.2, f32[256,1024]{1,0:T(8,128)S(1)} %fusion.1, f32[2,1024,256]{2,1,0:T(8,128)S(1)} %copy-done.1), kind=kOutput, calls=%fused_computation.1 | convolution fusion | flops 3222274048 | bytes 10485760 | tf_op jit(solution)/shard_map/dot_general | solution.py:10
  227.3 0.0 copy-start
  227.3 2.0 copy-done
  229.3 7.8 %convolution_bitcast_fusion = f32[256,1024]{0,1:T(8,128)} fusion(f32[1024,1024]{1,0:T(8,128)S(1)} %bitcast_subtract_fusion.1, f32[2,1024,256]{2,1,0:T(8,128)S(1)} %copy-done.1), kind=kOutput, calls=%fused_computation.2 | convolution fusion | flops 3221225472 | bytes 6291456 | tf_op jit(solution)/shard_map/dot_general | solution.py:10
  237.1 0.0 all-reduce.6.cloned.1.call-update
  237.2 58.5 %all-reduce.6.cloned.1.call-done = f32[256,1024]{0,1:T(8,128)} async-done(((f32[256,1024]{0,1:T(8,128)}), f32[256,1024]{0,1:T(8,128)}) %all-reduce.6.cloned.1.call-update) | async-done | bytes 1048592 | tf_op jit(solution)/shard_map/psum | solution.py:24
  295.6 2.3 fusion
  297.9 6.7 %bitcast_subtract_fusion = f32[1024,1024]{1,0:T(8,128)} fusion(f32[1024,1024]{1,0:T(8,128)} %copy-done, f32[256,1024]{1,0:T(8,128)S(1)} %fusion, f32[2,1024,256]{2,1,0:T(8,128)S(1)} %copy-done.1), kind=kOutput, calls=%fused_computation | convolution fusion | flops 3222274048 | bytes 10485760 | tf_op jit(solution)/shard_map/dot_general | solution.py:10
  304.6 0.0 copy-start.2
  304.6 0.0 copy-start.3
  304.6 5.0 %all-to-all-start = ((f32[4,256,1024]{2,1,0:T(8,128)}), f32[4,256,1024]{2,1,0:T(8,128)}, u32[]{:S(2)}, u32[]{:S(2)}) async-start(f32[4,256,1024]{2,1,0:T(8,128)} %bitcast.40), calls=%async_computation | async-start | bytes 8388608 | tf_op jit(solution)/shard_map/all_to_all | solution.py:14
  309.5 0.0 copy-done.2
  309.6 0.2 reduce_sum.18
  309.7 0.0 copy-done.3
  309.7 0.2 reduce_sum.19
  309.9 48.7 %all-reduce = (f32[1,256]{1,0:T(1,128)S(1)}, f32[1,256]{1,0:T(1,128)S(1)}) all-reduce(f32[1,256]{1,0:T(1,128)S(1)} %bitcast.45, f32[1,256]{1,0:T(1,128)S(1)} %bitcast.44), channel_id=1, replica_groups=mesh['row'=8,'col'=4] {'col'}, use_global_device_ids=true, to_apply=%region_5.6 | all-reduce | flops 512 | bytes 4096 | tf_op jit(solution)/shard_map/psum | solution.py:35
  358.5 0.6 maximum_multiply_fusion
  359.1 0.0 all-to-all-done
  359.1 4.8 %copy.10 = f32[4,32,8,1024]{3,2,0,1:T(8,128)} copy(f32[4,32,8,1024]{3,2,1,0:T(8,128)} %bitcast.16) | data formatting | bytes 8388608 | tf_op jit(solution)/shard_map/all_to_all | solution.py:14
  (1 shorter events, 0.0 us)
Async XLA Ops:
  7.2 58.0 %all-gather.9.cloned.1.call-start = ((), (), s32[]{:S(2)}) async-start(), calls=%async_computation.5 | async-start | bytes 5242880 | tf_op jit(solution)/shard_map/all_gather | solution.py:19
  7.9 105.7 %all-gather.5.cloned.1.call-start = ((), (), s32[]{:S(2)}) async-start(), calls=%async_computation.1 | async-start | bytes 4718592 | tf_op jit(solution)/shard_map/all_gather | solution.py:18
  8.6 140.9 %all-gather.7.cloned.1.call-start = ((), (), s32[]{:S(2)}) async-start(), calls=%async_computation.2 | async-start | bytes 2621440 | tf_op jit(solution)/shard_map/all_gather | solution.py:21
  9.4 209.9 %all-reduce.4.cloned.1.call-start = ((), (), s32[]{:S(2)}) async-start(), calls=%async_computation.3 | async-start | bytes 2097152 | tf_op jit(solution)/shard_map/psum | solution.py:24
  131.2 28.8 %copy-start.4 = (f32[2,256,256]{2,1,0:T(8,128)S(1)}, f32[2,256,256]{2,1,0:T(8,128)}, u32[]{:S(2)}) copy-start(f32[2,256,256]{2,1,0:T(8,128)} %param.7) | copy-start | bytes 1572868
  149.5 72.0 %copy-start.1 = (f32[2,1024,256]{2,1,0:T(8,128)S(1)}, f32[2,1024,256]{2,1,0:T(8,128)}, u32[]{:S(2)}) copy-start(f32[2,1024,256]{2,1,0:T(8,128)} %all-gather.7.cloned.1.call-done) | copy-start | bytes 6291460
  159.8 135.8 %all-reduce.6.cloned.1.call-start = ((), (), s32[]{:S(2)}) async-start(), calls=%async_computation.4 | async-start | bytes 2097152 | tf_op jit(solution)/shard_map/psum | solution.py:24
  227.3 2.0 copy-start
  304.6 5.0 %copy-start.2 = (f32[256,1024]{0,1:T(8,128)S(1)}, f32[256,1024]{0,1:T(8,128)}, u32[]{:S(2)}) copy-start(f32[256,1024]{0,1:T(8,128)} %all-reduce.4.cloned.1.call-done) | copy-start | bytes 3145732
  304.6 5.1 %copy-start.3 = (f32[256,1024]{0,1:T(8,128)S(1)}, f32[256,1024]{0,1:T(8,128)}, u32[]{:S(2)}) copy-start(f32[256,1024]{0,1:T(8,128)} %all-reduce.6.cloned.1.call-done) | copy-start | bytes 3145732
  304.6 54.6 %all-to-all-start = ((f32[4,256,1024]{2,1,0:T(8,128)}), f32[4,256,1024]{2,1,0:T(8,128)}, u32[]{:S(2)}, u32[]{:S(2)}) async-start(f32[4,256,1024]{2,1,0:T(8,128)} %bitcast.40), calls=%async_computation | async-start | bytes 8388608 | tf_op jit(solution)/shard_map/all_to_all | solution.py:14
Sparse Core Ops, SparseCore 0:
  9.8 55.2 all-gather.8
  66.7 46.8 all-gather.4
  115.5 33.9 all-gather.6
  159.9 59.2 all-reduce.3
  237.3 58.2 all-reduce.5
